TPU v7x, 32 devices: a 4x2x2 block of a 4x4x8 slice. The times are simulated.
32 devices in a mesh: data: 4 (over y, z), expert: 8 (over x, core).
Axes of the slice: x: 4, y: 2, z: 2, core: 2. Of those that a mesh axis runs over, the one named last changes fastest.
The devices are a block of a 4x4x8 slice.
Arguments:
- token_rows: bfloat16 [32768, 2304], P(('data', 'expert')), parts along dimension 0
- expert_ids: int32 [32768, 2], P(('data', 'expert')), parts along dimension 0
- gate_weights: float32 [32768, 2], P(('data', 'expert')), parts along dimension 0
- w_in: bfloat16 [8, 2304, 5760], P('expert')
- w_out: bfloat16 [8, 5760, 2304], P('expert')
Outputs:
- output: bfloat16 [32768, 2304], P(('data', 'expert')), parts along dimension 0
There are 4 independent parts. A program takes and returns all parts, laid end to end along the dimension named above; an argument that names none is the same for every part.
All inputs are finite; a program needn't handle non-finite values.
Results may differ from a plain program's by a relative error of at most 0.001.
Values are sent between devices in bfloat16 or wider.
A program may use at most 768 MiB of HBM per device.

v0:
```python
import jax
import jax.numpy as jnp
from jax import lax
from jax.sharding import PartitionSpec as P


def route_local(expert_ids, experts):
    ids_t = expert_ids.T
    onehot = (ids_t[:, :, None] == jnp.arange(experts, dtype=jnp.int32)).astype(jnp.int32)
    running = jnp.cumsum(onehot, axis=1)
    counts = running[:, -1, :]
    rank_local = jnp.sum(onehot * running, axis=2) - 1
    return ids_t, counts, rank_local


def solution(mesh):
    groups = mesh.shape["expert"]
    row_spec = P(("data", "expert"), None)
    weight_spec = P("expert", None, None)

    def device_step(token_rows, expert_ids, gate_weights, w_in, w_out):
        tokens, top_k = expert_ids.shape
        local_experts, model_dim = w_in.shape[0], w_in.shape[1]
        experts = local_experts * groups
        mean_load = tokens * top_k // experts
        send_cap = 7 * mean_load // 4
        capacity = groups * mean_load
        rows_total = experts * send_cap
        ids_t, counts, rank_local = route_local(expert_ids, experts)
        inclusive = counts
        shift = 1
        while shift < groups:
            pairs_list = [(source, source + shift) for source in range(groups - shift)]
            inclusive = inclusive + lax.ppermute(inclusive, "expert", pairs_list)
            shift = shift * 2
        before = inclusive - counts
        totals = lax.psum(counts, "expert")
        prior = jnp.cumsum(totals, axis=0) - totals
        within = jnp.cumsum(counts, axis=0) - counts
        slot = jnp.take_along_axis(prior + before, ids_t, axis=1) + rank_local
        keep = slot < capacity
        target = ids_t * send_cap + jnp.take_along_axis(within, ids_t, axis=1) + rank_local
        token_ids = jnp.broadcast_to(jnp.arange(tokens, dtype=jnp.int32), (top_k, tokens))
        source_row = jnp.full((rows_total,), tokens, jnp.int32).at[jnp.where(keep, target, rows_total).reshape(-1)].set(token_ids.reshape(-1), mode="drop")
        padded = jnp.concatenate([token_rows, jnp.zeros((1, model_dim), token_rows.dtype)], axis=0)
        outbound = jnp.take(padded, source_row, axis=0).reshape(experts, send_cap, model_dim)
        inbound = lax.all_to_all(outbound, "expert", 0, 0, tiled=True).reshape(groups, local_experts, send_cap, model_dim)
        pre_act = jnp.einsum("gesd,edf->gesf", inbound, w_in, preferred_element_type=jnp.float32)
        hidden = jax.nn.gelu(pre_act).astype(jnp.bfloat16)
        expert_out = jnp.einsum("gesf,efd->gesd", hidden, w_out, preferred_element_type=jnp.float32).astype(jnp.bfloat16)
        returned = lax.all_to_all(expert_out.reshape(experts, send_cap, model_dim), "expert", 0, 0, tiled=True).reshape(rows_total, model_dim)
        picked = jnp.take(returned, target, axis=0)
        weight = jnp.where(keep, gate_weights.T, 0.0)
        mixed = jnp.sum(weight[:, :, None] * picked.astype(jnp.float32), axis=0)
        return (token_rows.astype(jnp.float32) + mixed).astype(jnp.bfloat16)

    return jax.shard_map(device_step, mesh=mesh, in_specs=(row_spec, row_spec, row_spec, weight_spec, weight_spec), out_specs=row_spec, check_vma=False)
```

profile of v0, /device:TPU:81, one launch (start us, length us, event | category | flops | bytes accessed | tf_op | source)
XLA Modules:
  0.0 790.4 jit_solution(10942422809443658839)
XLA Ops:
  0.0 0.8 copy.43
  0.8 4.5 reduce-window.6
  6.6 4.6 collective-permute-start
  11.2 0.7 fusion.26
  11.9 7.2 psum.7
  19.2 0.9 copy.29
  20.1 20.9 %fusion.24 = s32[2,1024]{0,1:T(8,128)S(1)} fusion(s32[2,1024,8]{2,0,1:T(2,128)S(1)} %bitcast.108, s32[2,1024]{0,1:T(8,128)S(1)} %copy.29), kind=kLoop, calls=%fused_computation.27 | loop fusion | flops 47104 | bytes 81920 | tf_op jit(solution)/shard_map/reduce_sum | solution.py:12
  41.2 4.8 concatenate.3
  46.0 2.1 collective-permute-start.1
  48.1 17.6 %gather_fusion.3 = s32[2048]{0:T(1024)S(1)} fusion(s32[2,8]{1,0:T(2,128)S(1)} %get-tuple-element.10, s32[2048]{0:T(1024)S(1)} %bitcast.103), kind=kCustom, calls=%fused_computation.1.clone | custom fusion | bytes 32768 | tf_op jit(solution)/shard_map/jit(take_along_axis)/gather | solution.py:42
  65.7 3.6 collective-permute-start.2
  69.3 0.6 compare_and_fusion.2
  70.1 17.5 %gather_fusion.2 = s32[2048]{0:T(1024)S(1)} fusion(s32[2,8]{1,0:T(2,128)S(1)} %subtract_add_fusion, s32[2048]{0:T(1024)S(1)} %bitcast.104), kind=kCustom, calls=%fused_computation.clone | custom fusion | bytes 32768 | tf_op jit(solution)/shard_map/jit(take_along_axis)/gather | solution.py:40
  88.9 8.1 %scatter_custom_fusion = s32[3584]{0:T(1024)S(1)} fusion(s32[2048]{0:T(1024)S(1)} %bitcast.117, s32[2048]{0:T(1024)S(1)} %bitcast.116, s32[]{:T(128)} %constant.44.clone.1), kind=kCustom, calls=%fused_computation.53 | custom fusion | bytes 14340 | tf_op jit(solution)/shard_map/scatter | solution.py:44
  97.1 33.9 %gather_fusion = bf16[3584,2304]{1,0:T(8,128)(2,1)} fusion(bf16[1025,2304]{1,0:T(8,128)(2,1)} %concatenate.3, s32[4096]{0:T(1024)S(1)} %pad_clamp_fusion), kind=kCustom, calls=%fused_computation.2 | custom fusion | bytes 33044480 | tf_op jit(solution)/shard_map/jit(_take)/gather | solution.py:46
  131.0 8.4 %broadcast_select_fusion = bf16[8,448,2304]{2,1,0:T(8,128)(2,1)S(1)} fusion(bf16[8,448,2304]{2,1,0:T(8,128)(2,1)} %bitcast.105, pred[8,448]{1,0:T(8,128)(4,1)S(1)} %broadcast_in_dim.50), kind=kLoop, calls=%fused_computation.24 | loop fusion | flops 8257536 | bytes 33033728 | tf_op jit(solution)/shard_map/jit(_take)/select_n | solution.py:46
  139.5 188.3 %all_to_all.10 = bf16[8,448,2304]{2,1,0:T(8,128)(2,1)} all-to-all(bf16[8,448,2304]{2,1,0:T(8,128)(2,1)S(1)} %broadcast_select_fusion), channel_id=1, replica_groups=mesh['data'=4,'expert'=8] {'expert'}, dimensions={0} | all-to-all | bytes 33030144 | tf_op jit(solution)/shard_map/all_to_all | solution.py:47
  327.8 121.5 %fusion.50 = bf16[8,448,5760]{2,1,0:T(8,128)(2,1)} fusion(bf16[8,448,2304]{2,1,0:T(8,128)(2,1)} %all_to_all.10, bf16[1,2304,5760]{2,1,0:T(8,128)(2,1)} %param.10), kind=kOutput, calls=%fused_computation.15.clone.clone.clone.1 | convolution fusion | flops 95312609280 | bytes 84344832 | tf_op jit(solution)/shard_map/gesd,edf->gesf/dot_general | solution.py:48
  449.3 108.1 %fusion.17 = bf16[8,448,2304]{2,1,0:T(8,128)(2,1)} fusion(bf16[1,5760,2304]{2,1,0:T(8,128)(2,1)} %param.11, bf16[8,448,5760]{2,1,0:T(8,128)(2,1)} %fusion.50), kind=kOutput, calls=%fused_computation.22 | convolution fusion | flops 95135072256 | bytes 84344832 | tf_op jit(solution)/shard_map/gesf,efd->gesd/dot_general | solution.py:50
  557.4 6.8 all-to-all-start.1
  564.2 180.7 %all-to-all-done.1 = bf16[8,448,2304]{2,1,0:T(8,128)(2,1)} async-done(((bf16[8,448,2304]{2,1,0:T(8,128)(2,1)}), bf16[8,448,2304]{2,1,0:T(8,128)(2,1)}, u32[]{:S(2)}, u32[]{:S(2)}) %all-to-all-start.1) | async-done | bytes 16515104 | tf_op jit(solution)/shard_map/all_to_all | solution.py:51
  744.9 26.1 %gather_fusion.1 = bf16[2048,2304]{1,0:T(8,128)(2,1)} fusion(bf16[3584,2304]{1,0:T(8,128)(2,1)} %bitcast.20, s32[2048]{0:T(1024)S(1)} %bitcast_clamp_fusion), kind=kCustom, calls=%fused_computation.3 | custom fusion | bytes 18882560 | tf_op jit(solution)/shard_map/jit(_take)/gather | solution.py:52
  771.0 13.6 %multiply_reduce_fusion = f32[1024,2304]{1,0:T(8,128)S(1)} fusion(bf16[2,1024,2304]{2,1,0:T(8,128)(2,1)} %bitcast.106, f32[2,1024]{1,0:T(2,128)S(1)} %copy-done.1, pred[2,1024]{1,0:T(4,128)(4,1)S(1)} %copy-done.3), kind=kLoop, calls=%fused_computation.23 | loop fusion | flops 16515072 | bytes 18884608 | tf_op jit(solution)/shard_map/reduce_sum | solution.py:54
  784.6 5.8 add_convert_fusion
  (39 shorter events, 3.0 us)
Async XLA Ops:
  0.0 69.3 %copy-start = (s32[1024,2]{0,1:T(2,128)S(1)}, s32[1024,2]{0,1:T(2,128)}, u32[]{:S(2)}) copy-start(s32[1024,2]{0,1:T(2,128)} %param.8) | copy-start | bytes 24580
  5.3 82.3 %copy-start.4 = (f32[1024,2]{0,1:T(2,128)S(1)}, f32[1024,2]{0,1:T(2,128)}, u32[]{:S(2)}) copy-start(f32[1024,2]{0,1:T(2,128)} %param.9) | copy-start | bytes 24580
  6.6 39.4 %collective-permute-start = (s32[2,8]{1,0:T(2,128)S(1)}, s32[2,8]{1,0:T(2,128)S(1)}, u32[]{:S(2)}, u32[]{:S(2)}) collective-permute-start(s32[2,8]{1,0:T(2,128)S(1)} %slice_bitcast_fusion), channel_id=1, source_target_pairs={{0,1},{1,2},{2,3},{3,4},{4,5},{5,6},{6,7},{8,9},{9,10},{10,11},{11... | collective-permute-start | bytes 200 | tf_op jit(solution)/shard_map/ppermute | solution.py:34
  46.0 19.7 %collective-permute-start.1 = (s32[2,8]{1,0:T(2,128)S(1)}, s32[2,8]{1,0:T(2,128)S(1)}, u32[]{:S(2)}, u32[]{:S(2)}) collective-permute-start(s32[2,8]{1,0:T(2,128)S(1)} %get-tuple-element.11), channel_id=1, source_target_pairs={{0,2},{1,3},{2,4},{3,5},{4,6},{5,7},{8,10},{9,11},{10,12},{11,13},... | collective-permute-start | bytes 200 | tf_op jit(solution)/shard_map/ppermute | solution.py:34
  65.7 4.3 collective-permute-start.2
  557.4 6.8 copy-start.2
  557.4 187.5 %all-to-all-start.1 = ((bf16[8,448,2304]{2,1,0:T(8,128)(2,1)}), bf16[8,448,2304]{2,1,0:T(8,128)(2,1)}, u32[]{:S(2)}, u32[]{:S(2)}) async-start(bf16[8,448,2304]{2,1,0:T(8,128)(2,1)} %fusion.17), calls=%async_computation.1 | async-start | bytes 33030144 | tf_op jit(solution)/shard_map/all_to_all | solution.py:51
  744.9 26.1 %copy-start.1 = (f32[2,1024]{1,0:T(2,128)S(1)}, f32[2,1024]{1,0:T(2,128)}, u32[]{:S(2)}) copy-start(f32[2,1024]{1,0:T(2,128)} %get-tuple-element.8) | copy-start | bytes 24580
  744.9 26.1 %copy-start.3 = (pred[2,1024]{1,0:T(4,128)(4,1)S(1)}, pred[2,1024]{1,0:T(4,128)(4,1)}, u32[]{:S(2)}) copy-start(pred[2,1024]{1,0:T(4,128)(4,1)} %get-tuple-element.6) | copy-start | bytes 6148
where the time goes:
time: 791 us; the launch traced here: 790 us
  matrix products  230 us (29%)
  blocking collectives  196 us (25%)
  waiting for transfers between devices  181 us (23%)
  local copies, waits for them, and re-layouts  111 us (14%)
  other arithmetic  56.4 us (7%)
  starting transfers between devices  17.1 us (2%)
    all_to_all x1, blocking collectives, device_step(): lax.all_to_all(outbound, 'expert', 0, 0, tiled=True)  188 us
    all_to_all x1, waiting for transfers between devices, device_step(): lax.all_to_all(expert_out.reshape(experts, send_cap, model_dim), 'expert'...  181 us
    dot_general x1, matrix products, device_step(): jnp.einsum('gesd,edf->gesf', inbound, w_in, preferred_element_type=jnp.fl...  121 us
    dot_general x1, matrix products, device_step(): jnp.einsum('gesf,efd->gesd', hidden, w_out, preferred_element_type=jnp.fl...  108 us
    gather x1, local copies, waits for them, and re-layouts, device_step(): jnp.take(padded, source_row, axis=0).reshape(experts, send_cap, model_dim)  33.9 us
    gather x1, local copies, waits for them, and re-layouts, device_step(): picked = jnp.take(returned, target, axis=0)  26.1 us
    reduce_sum x1, other arithmetic, route_local(): rank_local = jnp.sum(onehot * running, axis=2) - 1  20.9 us
    gather x2, local copies, waits for them, and re-layouts, device_step(): jnp.take_along_axis(within, ids_t, axis=1)  17.6 us
  transfers between devices with their start and end apart: 4, of which 2 were waited for; matrix products, arithmetic and copies ran while one was open for 6% of the time, Pallas kernels for 0%

commit v1 on v0

v1 whole, which is shorter than its diff:
```python
import functools

import jax
import jax.numpy as jnp
from jax import lax
from jax.experimental import pallas as pl
from jax.experimental.pallas import tpu as pltpu
from jax.sharding import PartitionSpec as P

MESH = pl.DeviceIdType.MESH
F32 = jnp.float32
BF16 = jnp.bfloat16


def layer_kernel(cfg, x_ref, ids_ref, gates_ref, win_ref, wout_ref, out_ref, ag_ref, obuf_ref, rbuf_ref,
                 ids_all, slot_tab, comb_tab, ids_send, ids_recv, ag_send, ag_recv, ret_send, ret_recv, barrier_unused=None):
    groups, tokens, dim, hid, cap, slots = cfg
    half = tokens // 2
    chips = groups // 2
    wchunk = 768
    nfull = hid // wchunk
    tail = hid - nfull * wchunk
    ochunks = dim // wchunk

    me = lax.axis_index("expert")
    chip = me // 2
    core = me % 2
    other = 1 - core
    sgn = 1 - 2 * core

    def dev(off, c):
        return ((chip + off + 2 * chips) % chips) * 2 + c

    sib = dev(0, other)
    src_a = dev(-sgn, core)
    src_b = dev(sgn, core)
    far = dev(2, core)

    def tile_dev(t, flip):
        q = t // 2
        p = t % 2
        f1 = q * (2 - q) * (3 - q) // 2
        f2 = q * (q - 1) * (3 - q) // 2
        f3 = q * (q - 1) * (q - 2) // 6
        off = flip * (f1 * (2 * p - 1) + f2 * (1 - 2 * p)) * sgn + 2 * f3
        c = core * (1 - p) + other * p
        return dev(off, c)

    def comb_dev(k):
        q = k // 2
        p = k % 2
        f1 = q * (2 - q) * (3 - q) // 2
        f2 = q * (q - 1) * (3 - q) // 2
        f3 = q * (q - 1) * (q - 2) // 6
        off = (f1 - f2) * sgn + 2 * f3
        c = core * (1 - p) + other * p
        return dev(off, c)

    def remote(src, dst, ssem, rsem, target):
        return pltpu.make_async_remote_copy(src_ref=src, dst_ref=dst, send_sem=ssem, recv_sem=rsem,
                                            device_id={"expert": target}, device_id_type=MESH)

    bar = pltpu.get_barrier_semaphore()
    for k in range(1, groups):
        pl.semaphore_signal(bar, inc=1, device_id={"expert": (me + k) % groups}, device_id_type=MESH)
    pl.semaphore_wait(bar, groups - 1)

    def ids_copy(k):
        return remote(ids_ref, ids_all.at[me], ids_send.at[k - 1], ids_recv.at[me], (me + k) % groups)

    def ag_copy(src, d, h, k, target):
        return remote(src, ag_ref.at[d, pl.ds(h * half, half)], ag_send.at[k], ag_recv.at[2 * d + h], target)

    def own_half(h):
        return x_ref.at[pl.ds(h * half, half)]

    def got_half(d, h):
        return ag_ref.at[d, pl.ds(h * half, half)]

    half_a = (1 - sgn) // 2
    half_b = 1 - half_a
    send_sib = [ag_copy(own_half(h), me, h, h, sib) for h in range(2)]
    send_a = [ag_copy(own_half(h), me, h, 2 + h, src_b) for h in range(2)]
    send_b = [ag_copy(own_half(h), me, h, 4 + h, src_a) for h in range(2)]
    fwd_a = ag_copy(got_half(src_a, half_a), src_a, half_a, 6, src_b)
    fwd_b = ag_copy(got_half(src_b, half_b), src_b, half_b, 7, src_a)
    pass_a = [ag_copy(got_half(src_a, h), src_a, h, 8 + h, sib) for h in range(2)]
    pass_b = [ag_copy(got_half(src_b, h), src_b, h, 10 + h, sib) for h in range(2)]
    pass_f = [ag_copy(got_half(far, h), far, h, 12 + h, sib) for h in range(2)]
    all_sends = send_sib + send_a + send_b + [fwd_a, fwd_b] + pass_a + pass_b + pass_f

    def wait_half(d, h):
        ag_copy(got_half(d, h), d, h, 0, sib).wait_recv()

    def ret_copy(t):
        d = tile_dev(t, 1)
        return remote(obuf_ref.at[d], rbuf_ref.at[me], ret_send.at[t], ret_recv.at[me], d)

    for k in range(1, groups):
        ids_copy(k).start()
    for c in send_sib + send_a:
        c.start()

    def compute(xsrc, xg, hbuf, wbuf, wout, ostage, pbuf, xsem, wsem, osem, stsem, isem):
        own_ids = pltpu.make_async_copy(ids_ref, ids_all.at[me], isem)
        own_ids.start()

        def win_full(i):
            return pltpu.make_async_copy(win_ref.at[:, pl.ds(pl.multiple_of(i * wchunk, 128), wchunk)], wbuf.at[i % 2], wsem.at[i % 2])

        win_tail = pltpu.make_async_copy(win_ref.at[:, pl.ds(nfull * wchunk, tail)], wbuf.at[nfull % 2, :, pl.ds(0, tail)], wsem.at[nfull % 2])

        def wout_part(n):
            return pltpu.make_async_copy(wout_ref.at[:, pl.ds(pl.multiple_of(n * wchunk, 128), wchunk)], wout.at[:, pl.ds(pl.multiple_of(n * wchunk, 128), wchunk)], osem.at[n])

        win_full(0).start()
        for n in range(ochunks):
            wout_part(n).start()

        own_ids.wait()
        for k in range(1, groups):
            ids_copy(k).wait_send()
        for k in range(1, groups):
            d = (me + k) % groups
            remote(ids_ref, ids_all.at[d], ids_send.at[0], ids_recv.at[d], sib).wait_recv()
        ids0 = ids_all[:, 0, :]
        ids1 = ids_all[:, 1, :]
        o0 = ids_ref_v(ids_all, me, 0)
        o1 = ids_ref_v(ids_all, me, 1)
        eidx = lax.broadcasted_iota(jnp.int32, (groups, tokens), 0)

        def ind(m):
            return jnp.where(m, 1.0, 0.0).astype(F32)

        m0 = ind(ids0 == me)
        m1 = ind(ids1 == me)
        n0 = ind(o0 == eidx)
        n1 = ind(o1 == eidx)
        stack = jnp.concatenate([m0, m1, n0, n1], axis=0).astype(BF16)
        tri = ind(lax.broadcasted_iota(jnp.int32, (tokens, tokens), 0) < lax.broadcasted_iota(jnp.int32, (tokens, tokens), 1)).astype(BF16)
        pre = jnp.dot(stack, tri, preferred_element_type=F32)
        s0, s1, r0, r1 = [pre[k * groups:(k + 1) * groups] for k in range(4)]
        c0 = jnp.sum(m0, axis=1, keepdims=True)
        c1 = jnp.sum(m1, axis=1, keepdims=True)
        k0 = jnp.sum(n0, axis=1, keepdims=True)
        run0 = jnp.zeros((1, 1), F32)
        run1 = jnp.zeros((1, 1), F32)
        b0 = []
        b1 = []
        for d in range(groups):
            b0.append(run0)
            b1.append(run1)
            run0 = run0 + c0[d:d + 1]
            run1 = run1 + c1[d:d + 1]
        before0 = jnp.concatenate(b0, axis=0)
        before1 = jnp.concatenate(b1, axis=0) + run0
        keep0 = jnp.logical_and(m0 > 0, before0 + s0 < cap)
        keep1 = jnp.logical_and(m1 > 0, before1 + s1 < cap)
        slot_tab[...] = jnp.where(keep0, s0, jnp.where(keep1, c0 + s1, -1.0))

        dmask = ind(eidx < me)
        g0 = []
        g1 = []
        for e in range(groups):
            a0 = ind(ids0 == e)
            a1 = ind(ids1 == e)
            g0.append(jnp.sum(jnp.sum(a0 * dmask, axis=1, keepdims=True), axis=0, keepdims=True))
            g1.append(jnp.sum(jnp.sum(a0 + a1 * dmask, axis=1, keepdims=True), axis=0, keepdims=True))
        own0 = jnp.logical_and(n0 > 0, jnp.concatenate(g0, axis=0) + r0 < cap)
        own1 = jnp.logical_and(n1 > 0, jnp.concatenate(g1, axis=0) + r1 < cap)
        slot_own = jnp.where(own0, r0, jnp.where(own1, k0 + r1, -1.0))
        gate_own = n0 * gates_ref[0:1, :] + n1 * gates_ref[1:2, :]
        both = jnp.concatenate([slot_own, gate_own, jnp.zeros((128 - 2 * groups, tokens), F32)], axis=0)
        comb_tab[...] = jnp.transpose(both)

        def stage_copy_own():
            return pltpu.make_async_copy(ostage, rbuf_ref.at[me], stsem)

        def stage_copy(t):
            return pltpu.make_async_copy(ostage, obuf_ref.at[tile_dev(t, 1)], stsem)

        def tile(t, carry):
            d = tile_dev(t, 1)

            @pl.when(t % 2 == 1)
            def _():
                wait_half(d, 0)
                wait_half(d, 1)

            def xcols(n):
                return pl.ds(pl.multiple_of(n * wchunk, 128), wchunk)

            def x_start(n):
                @pl.when(t == 0)
                def _():
                    pltpu.make_async_copy(x_ref.at[:, xcols(n)], xsrc.at[n % 2], xsem.at[n % 2]).start()

                @pl.when(t > 0)
                def _():
                    pltpu.make_async_copy(ag_ref.at[d, :, xcols(n)], xsrc.at[n % 2], xsem.at[n % 2]).start()

            x_start(0)
            row = slot_tab[pl.ds(d, 1), :]
            pbuf[...] = jnp.where(lax.broadcasted_iota(jnp.int32, (slots, tokens), 0).astype(F32) == row, 1.0, 0.0).astype(BF16)

            def gather(n, cc):
                @pl.when(n + 1 < ochunks)
                def _():
                    x_start(n + 1)
                pltpu.make_async_copy(x_ref.at[:, xcols(n)], xsrc.at[n % 2], xsem.at[n % 2]).wait()
                xg[:, xcols(n)] = jnp.dot(pbuf[...], xsrc[n % 2], preferred_element_type=F32).astype(BF16)
                return cc

            lax.fori_loop(0, ochunks, gather, 0)

            def up(i, cc):
                @pl.when(jnp.logical_and(t == 1, i == 0))
                def _():
                    wait_half(src_a, 0)
                    pass_a[0].start()

                @pl.when(jnp.logical_and(t == 1, i == 1))
                def _():
                    stage_copy_own().wait()

                @pl.when(jnp.logical_and(t > 1, i == 1))
                def _():
                    stage_copy(t - 1).wait()

                    @pl.when(t != 3)
                    def _():
                        ret_copy(t - 1).start()

                @pl.when(i + 1 < nfull)
                def _():
                    win_full(i + 1).start()

                @pl.when(i + 1 == nfull)
                def _():
                    win_tail.start()

                win_full(i).wait()
                pre_act = jnp.dot(xg[...], wbuf[i % 2], preferred_element_type=F32)
                hbuf[:, pl.ds(pl.multiple_of(i * wchunk, 128), wchunk)] = jax.nn.gelu(pre_act).astype(BF16)
                return cc

            lax.fori_loop(0, nfull, up, 0)
            win_tail.wait()

            @pl.when(t + 1 < groups)
            def _():
                win_full(0).start()
            pre_act = jnp.dot(xg[...], wbuf[nfull % 2, :, 0:tail], preferred_element_type=F32)
            hbuf[:, nfull * wchunk:hid] = jax.nn.gelu(pre_act).astype(BF16)

            def down(n, cc):
                @pl.when(t == 0)
                def _():
                    wout_part(n).wait()

                @pl.when(jnp.logical_and(t == 1, n == 1))
                def _():
                    wait_half(src_a, 1)
                    pass_a[1].start()
                    send_b[0].start()
                    send_b[1].start()

                @pl.when(jnp.logical_and(t == 2, n == 1))
                def _():
                    wait_half(src_b, 0)
                    pass_b[0].start()

                @pl.when(jnp.logical_and(t == 3, n == 0))
                def _():
                    wait_half(src_b, 1)
                    fwd_a.start()
                    fwd_b.start()
                    pass_b[1].start()
                    ret_copy(2).start()

                @pl.when(jnp.logical_and(t == 5, n == 0))
                def _():
                    wait_half(far, 0)
                    wait_half(far, 1)
                    pass_f[0].start()
                    pass_f[1].start()

                cols = pl.ds(pl.multiple_of(n * wchunk, 128), wchunk)
                ostage[:, cols] = jnp.dot(hbuf[...], wout[:, cols], preferred_element_type=F32).astype(BF16)
                return cc

            lax.fori_loop(0, ochunks, down, 0)

            @pl.when(t == 0)
            def _():
                stage_copy_own().start()

            @pl.when(t > 0)
            def _():
                stage_copy(t).start()
            return carry

        lax.fori_loop(0, groups, tile, 0)
        stage_copy(groups - 1).wait()
        ret_copy(groups - 1).start()

    def ids_ref_v(ref, d, j):
        return ref[pl.ds(d, 1), j, :]

    pl.run_scoped(
        compute,
        pltpu.VMEM((2, tokens, wchunk), BF16),
        pltpu.VMEM((slots, dim), BF16),
        pltpu.VMEM((slots, hid), BF16),
        pltpu.VMEM((2, dim, wchunk), BF16),
        pltpu.VMEM((hid, dim), BF16),
        pltpu.VMEM((slots, dim), BF16),
        pltpu.VMEM((slots, tokens), BF16),
        pltpu.SemaphoreType.DMA((2,)),
        pltpu.SemaphoreType.DMA((2,)),
        pltpu.SemaphoreType.DMA((ochunks,)),
        pltpu.SemaphoreType.DMA(()),
        pltpu.SemaphoreType.DMA(()),
    )

    def combine(acc, xb, rb, qbuf, xsem, rsem, osem):
        x_in = pltpu.make_async_copy(x_ref, xb, xsem)
        x_in.start()
        x_in.wait()
        for n in range(ochunks):
            cols = slice(n * wchunk, (n + 1) * wchunk)
            acc[:, cols] = xb[:, cols].astype(F32)

        def add_block(k, cc):
            e = comb_dev(k)

            @pl.when(k > 0)
            def _():
                remote(obuf_ref.at[e], rbuf_ref.at[e], ret_send.at[0], ret_recv.at[e], sib).wait_recv()
            cp = pltpu.make_async_copy(rbuf_ref.at[e], rb, rsem)
            cp.start()
            lane = lax.broadcasted_iota(jnp.int32, (tokens, 128), 1)
            tab = comb_tab[...]
            slot_col = jnp.sum(jnp.where(lane == e, tab, 0.0), axis=1, keepdims=True)
            gate_col = jnp.sum(jnp.where(lane == e + groups, tab, 0.0), axis=1, keepdims=True)
            qbuf[...] = jnp.where(lax.broadcasted_iota(jnp.int32, (tokens, slots), 1).astype(F32) == slot_col, 1.0, 0.0).astype(BF16)
            cp.wait()

            def part(n, c2):
                cols = pl.ds(pl.multiple_of(n * wchunk, 128), wchunk)
                pick = jnp.dot(qbuf[...], rb[:, cols], preferred_element_type=F32)
                acc[:, cols] = acc[:, cols] + gate_col * pick
                return c2

            return lax.fori_loop(0, ochunks, part, cc)

        lax.fori_loop(0, groups, add_block, 0)
        xb[...] = acc[...].astype(BF16)
        fin = pltpu.make_async_copy(xb, out_ref, osem)
        fin.start()
        fin.wait()

    pl.run_scoped(
        combine,
        pltpu.VMEM((tokens, dim), F32),
        pltpu.VMEM((tokens, dim), BF16),
        pltpu.VMEM((slots, dim), BF16),
        pltpu.VMEM((tokens, slots), BF16),
        pltpu.SemaphoreType.DMA(()),
        pltpu.SemaphoreType.DMA(()),
        pltpu.SemaphoreType.DMA(()),
    )

    for c in all_sends:
        c.wait_send()
    for t in range(1, groups):
        ret_copy(t).wait_send()


def solution(mesh):
    groups = mesh.shape["expert"]
    row_spec = P(("data", "expert"), None)
    weight_spec = P("expert", None, None)

    def device_step(token_rows, expert_ids, gate_weights, w_in, w_out):
        tokens, top_k = expert_ids.shape
        dim, hid = w_in.shape[1], w_in.shape[2]
        mean_load = tokens * top_k // groups
        slots = 7 * mean_load // 4
        cap = groups * mean_load
        any_spec = pl.BlockSpec(memory_space=pl.ANY)
        vmem_spec = pl.BlockSpec(memory_space=pltpu.VMEM)
        flops = 4 * groups * slots * dim * hid
        out = pl.pallas_call(
            functools.partial(layer_kernel, (groups, tokens, dim, hid, cap, slots)),
            out_shape=(
                jax.ShapeDtypeStruct((tokens, dim), BF16),
                jax.ShapeDtypeStruct((groups, tokens, dim), BF16),
                jax.ShapeDtypeStruct((groups, slots, dim), BF16),
                jax.ShapeDtypeStruct((groups, slots, dim), BF16),
            ),
            in_specs=[any_spec, any_spec, vmem_spec, any_spec, any_spec],
            out_specs=(any_spec, any_spec, any_spec, any_spec),
            scratch_shapes=[
                pltpu.VMEM((groups, top_k, tokens), jnp.int32),
                pltpu.VMEM((groups, tokens), F32),
                pltpu.VMEM((tokens, 128), F32),
                pltpu.SemaphoreType.DMA((groups,)),
                pltpu.SemaphoreType.DMA((groups,)),
                pltpu.SemaphoreType.DMA((16,)),
                pltpu.SemaphoreType.DMA((2 * groups,)),
                pltpu.SemaphoreType.DMA((groups,)),
                pltpu.SemaphoreType.DMA((groups,)),
            ],
            compiler_params=pltpu.CompilerParams(collective_id=0, has_side_effects=True, vmem_limit_bytes=67043328),
            cost_estimate=pl.CostEstimate(flops=flops, bytes_accessed=400000000, transcendentals=0),
            name="layer",
        )(token_rows, expert_ids.T, gate_weights.T, w_in.reshape(dim, hid), w_out.reshape(hid, dim))
        return out[0]

    return jax.shard_map(device_step, mesh=mesh, in_specs=(row_spec, row_spec, row_spec, weight_spec, weight_spec), out_specs=row_spec, check_vma=False)
```

time: 791 us -> 380 us (0.48)
  Pallas kernels: 0 us -> 373 us
  matrix products: 230 us -> 0 us
  blocking collectives: 196 us -> 0 us
  waiting for transfers between devices: 181 us -> 0 us
  local copies, waits for them, and re-layouts: 111 us -> 4.83 us
  other arithmetic: 56.4 us -> 0 us
  starting transfers between devices: 17.1 us -> 0 us
    pallas_call x0 -> x1, Pallas kernels: none -> 373 us  [device_step(): pl.pallas_call(functools.partial(layer_kernel, (groups, tokens, dim, hid,...]
    dot_general x2 -> x0, matrix products: 230 us -> none  [the longest x1 121 us: device_step(): jnp.einsum('gesd,edf->gesf', inbound, w_in, preferred_element_type=jnp.fl...]
    all_to_all x1 -> x0, blocking collectives: 188 us -> none  [device_step(): lax.all_to_all(outbound, 'expert', 0, 0, tiled=True)]
    all_to_all x1 -> x0, waiting for transfers between devices: 181 us -> none  [device_step(): lax.all_to_all(expert_out.reshape(experts, send_cap, model_dim), 'expert'...]
    gather x6 -> x0, local copies, waits for them, and re-layouts: 95.1 us -> none  [the longest x1 33.9 us: device_step(): jnp.take(padded, source_row, axis=0).reshape(experts, send_cap, model_dim)]
    reduce_sum x2 -> x0, other arithmetic: 34.5 us -> none  [the longest x1 20.9 us: route_local(): rank_local = jnp.sum(onehot * running, axis=2) - 1]
    ppermute x3 -> x0, starting transfers between devices: 10.3 us -> none  [device_step(): inclusive = inclusive + lax.ppermute(inclusive, 'expert', pairs_list)]
    select_n x4 -> x0, other arithmetic: 9.06 us -> none  [the longest x2 8.43 us: device_step(): jnp.take(padded, source_row, axis=0).reshape(experts, send_cap, model_dim)]
  transfers between devices with their start and end apart: 4 -> 0, of which waited for: 2 -> 0; matrix products, arithmetic and copies ran while one was open for 6% -> 0% of each run, Pallas kernels for 0% -> 0%
where the time goes in v1:
time: 380 us; the launch traced here: 377 us
  Pallas kernels  373 us (98%)
  local copies, waits for them, and re-layouts  4.83 us (1%)
    pallas_call x1, Pallas kernels, device_step(): pl.pallas_call(functools.partial(layer_kernel, (groups, tokens, dim, hid,...  373 us

profile of v1, /device:TPU:81, one launch (start us, length us, event | category | flops | bytes accessed | tf_op | source)
XLA Modules:
  0.0 377.5 jit_solution(912456223332262847)
XLA Ops:
  0.0 372.6 %layer.1 = (bf16[1024,2304]{1,0:T(8,128)(2,1)}, bf16[8,1024,2304]{2,1,0:T(8,128)(2,1)}, bf16[8,448,2304]{2,1,0:T(8,128)(2,1)}, bf16[8,448,2304]{2,1,0:T(8,128)(2,1)}) custom-call(bf16[1024,2304]{1,0:T(8,128)(2,1)} %x_ref.1, s32[2,1024]{1,0:T(2,128)} %bitcast.6, f32[2,1024]{1,0:T(2,128)} %bitcast.7, bf16[2304,5760]{1,0:T(8,128)(2,1)} %bitcast.4, ...), custom_call_target="tpu_custom_call" | custom-call | flops 190253629440 | bytes 400000000 | tf_op jit(solution)/shard_map/layer/pallas_call | solution.py:394
  372.6 4.8 %copy.7 = bf16[1024,2304]{1,0:T(8,128)(2,1)} copy(bf16[1024,2304]{1,0:T(8,128)(2,1)} %get-tuple-element.6) | data formatting | bytes 9437184

commit v2 on v1

--- a/solution.py
+++ b/solution.py
@@ -81,13 +81,16 @@
     half_b = 1 - half_a
     send_sib = [ag_copy(own_half(h), me, h, h, sib) for h in range(2)]
     send_a = [ag_copy(own_half(h), me, h, 2 + h, src_b) for h in range(2)]
-    send_b = [ag_copy(own_half(h), me, h, 4 + h, src_a) for h in range(2)]
+    send_b1 = ag_copy(own_half(half_b), me, half_b, 4, src_a)
+    send_b2 = ag_copy(own_half(half_a), me, half_a, 5, src_a)
     fwd_a = ag_copy(got_half(src_a, half_a), src_a, half_a, 6, src_b)
     fwd_b = ag_copy(got_half(src_b, half_b), src_b, half_b, 7, src_a)
     pass_a = [ag_copy(got_half(src_a, h), src_a, h, 8 + h, sib) for h in range(2)]
-    pass_b = [ag_copy(got_half(src_b, h), src_b, h, 10 + h, sib) for h in range(2)]
-    pass_f = [ag_copy(got_half(far, h), far, h, 12 + h, sib) for h in range(2)]
-    all_sends = send_sib + send_a + send_b + [fwd_a, fwd_b] + pass_a + pass_b + pass_f
+    pass_b1 = ag_copy(got_half(src_b, half_b), src_b, half_b, 10, sib)
+    pass_b2 = ag_copy(got_half(src_b, half_a), src_b, half_a, 11, sib)
+    pass_f1 = ag_copy(got_half(far, half_a), far, half_a, 12, sib)
+    pass_f2 = ag_copy(got_half(far, half_b), far, half_b, 13, sib)
+    all_sends = send_sib + send_a + [send_b1, send_b2, fwd_a, fwd_b] + pass_a + [pass_b1, pass_b2, pass_f1, pass_f2]
 
     def wait_half(d, h):
         ag_copy(got_half(d, h), d, h, 0, sib).wait_recv()
@@ -101,7 +104,7 @@
     for c in send_sib + send_a:
         c.start()
 
-    def compute(xsrc, xg, hbuf, wbuf, wout, ostage, pbuf, xsem, wsem, osem, stsem, isem):
+    def compute(xsrc, xg, hbuf, pact, wbuf, wout, ostage, pbuf, xsem, wsem, osem, stsem, isem):
         own_ids = pltpu.make_async_copy(ids_ref, ids_all.at[me], isem)
         own_ids.start()
 
@@ -214,14 +217,22 @@
             lax.fori_loop(0, ochunks, gather, 0)
 
             def up(i, cc):
-                @pl.when(jnp.logical_and(t == 1, i == 0))
-                def _():
+                @pl.when(jnp.logical_and(t == 1, i == 2))
+                def _():
+                    stage_copy_own().wait()
                     wait_half(src_a, 0)
                     pass_a[0].start()
 
-                @pl.when(jnp.logical_and(t == 1, i == 1))
-                def _():
-                    stage_copy_own().wait()
+                @pl.when(jnp.logical_and(t == 3, i == 3))
+                def _():
+                    wait_half(src_b, half_b)
+                    fwd_b.start()
+                    pass_b1.start()
+
+                @pl.when(jnp.logical_and(t == 4, i == 3))
+                def _():
+                    wait_half(far, half_a)
+                    pass_f1.start()
 
                 @pl.when(jnp.logical_and(t > 1, i == 1))
                 def _():
@@ -240,16 +251,21 @@
                     win_tail.start()
 
                 win_full(i).wait()
-                pre_act = jnp.dot(xg[...], wbuf[i % 2], preferred_element_type=F32)
-                hbuf[:, pl.ds(pl.multiple_of(i * wchunk, 128), wchunk)] = jax.nn.gelu(pre_act).astype(BF16)
+                prev = pl.ds(pl.multiple_of((i - 1) * wchunk, 128), wchunk)
+                hbuf[:, prev] = jax.nn.gelu(pact[(i - 1) % 2]).astype(BF16)
+                pact[i % 2] = jnp.dot(xg[...], wbuf[i % 2], preferred_element_type=F32)
                 return cc
 
-            lax.fori_loop(0, nfull, up, 0)
+            win_full(1).start()
+            win_full(0).wait()
+            pact[0] = jnp.dot(xg[...], wbuf[0], preferred_element_type=F32)
+            lax.fori_loop(1, nfull, up, 0)
             win_tail.wait()
 
             @pl.when(t + 1 < groups)
             def _():
                 win_full(0).start()
+            hbuf[:, (nfull - 1) * wchunk:nfull * wchunk] = jax.nn.gelu(pact[(nfull - 1) % 2]).astype(BF16)
             pre_act = jnp.dot(xg[...], wbuf[nfull % 2, :, 0:tail], preferred_element_type=F32)
             hbuf[:, nfull * wchunk:hid] = jax.nn.gelu(pre_act).astype(BF16)
 
@@ -258,32 +274,24 @@
                 def _():
                     wout_part(n).wait()
 
-                @pl.when(jnp.logical_and(t == 1, n == 1))
-                def _():
+                @pl.when(jnp.logical_and(t == 1, n == 0))
+                def _():
+                    send_b1.start()
+                    send_b2.start()
                     wait_half(src_a, 1)
+                    fwd_a.start()
                     pass_a[1].start()
-                    send_b[0].start()
-                    send_b[1].start()
-
-                @pl.when(jnp.logical_and(t == 2, n == 1))
-                def _():
-                    wait_half(src_b, 0)
-                    pass_b[0].start()
-
-                @pl.when(jnp.logical_and(t == 3, n == 0))
-                def _():
-                    wait_half(src_b, 1)
-                    fwd_a.start()
-                    fwd_b.start()
-                    pass_b[1].start()
+
+                @pl.when(jnp.logical_and(t == 3, n == 2))
+                def _():
+                    wait_half(src_b, half_a)
+                    pass_b2.start()
                     ret_copy(2).start()
 
                 @pl.when(jnp.logical_and(t == 5, n == 0))
                 def _():
-                    wait_half(far, 0)
-                    wait_half(far, 1)
-                    pass_f[0].start()
-                    pass_f[1].start()
+                    wait_half(far, half_b)
+                    pass_f2.start()
 
                 cols = pl.ds(pl.multiple_of(n * wchunk, 128), wchunk)
                 ostage[:, cols] = jnp.dot(hbuf[...], wout[:, cols], preferred_element_type=F32).astype(BF16)
@@ -312,6 +320,7 @@
         pltpu.VMEM((2, tokens, wchunk), BF16),
         pltpu.VMEM((slots, dim), BF16),
         pltpu.VMEM((slots, hid), BF16),
+        pltpu.VMEM((2, slots, wchunk), F32),
         pltpu.VMEM((2, dim, wchunk), BF16),
         pltpu.VMEM((hid, dim), BF16),
         pltpu.VMEM((slots, dim), BF16),
@@ -331,28 +340,41 @@
             cols = slice(n * wchunk, (n + 1) * wchunk)
             acc[:, cols] = xb[:, cols].astype(F32)
 
+        def block_copy(k):
+            return pltpu.make_async_copy(rbuf_ref.at[comb_dev(k)], rb.at[k % 2], rsem.at[k % 2])
+
+        def block_ready(k):
+            e = comb_dev(k)
+            remote(obuf_ref.at[e], rbuf_ref.at[e], ret_send.at[0], ret_recv.at[e], sib).wait_recv()
+            block_copy(k).start()
+
+        block_copy(0).start()
+
         def add_block(k, cc):
             e = comb_dev(k)
 
-            @pl.when(k > 0)
-            def _():
-                remote(obuf_ref.at[e], rbuf_ref.at[e], ret_send.at[0], ret_recv.at[e], sib).wait_recv()
-            cp = pltpu.make_async_copy(rbuf_ref.at[e], rb, rsem)
-            cp.start()
+            @pl.when(k < groups - 2)
+            def _():
+                block_ready(k + 1)
             lane = lax.broadcasted_iota(jnp.int32, (tokens, 128), 1)
             tab = comb_tab[...]
             slot_col = jnp.sum(jnp.where(lane == e, tab, 0.0), axis=1, keepdims=True)
             gate_col = jnp.sum(jnp.where(lane == e + groups, tab, 0.0), axis=1, keepdims=True)
             qbuf[...] = jnp.where(lax.broadcasted_iota(jnp.int32, (tokens, slots), 1).astype(F32) == slot_col, 1.0, 0.0).astype(BF16)
-            cp.wait()
+            block_copy(k).wait()
 
             def part(n, c2):
                 cols = pl.ds(pl.multiple_of(n * wchunk, 128), wchunk)
-                pick = jnp.dot(qbuf[...], rb[:, cols], preferred_element_type=F32)
+                pick = jnp.dot(qbuf[...], rb[k % 2, :, cols], preferred_element_type=F32)
                 acc[:, cols] = acc[:, cols] + gate_col * pick
                 return c2
 
-            return lax.fori_loop(0, ochunks, part, cc)
+            lax.fori_loop(0, ochunks, part, 0)
+
+            @pl.when(k == groups - 2)
+            def _():
+                block_ready(k + 1)
+            return cc
 
         lax.fori_loop(0, groups, add_block, 0)
         xb[...] = acc[...].astype(BF16)
@@ -364,10 +386,10 @@
         combine,
         pltpu.VMEM((tokens, dim), F32),
         pltpu.VMEM((tokens, dim), BF16),
-        pltpu.VMEM((slots, dim), BF16),
+        pltpu.VMEM((2, slots, dim), BF16),
         pltpu.VMEM((tokens, slots), BF16),
         pltpu.SemaphoreType.DMA(()),
-        pltpu.SemaphoreType.DMA(()),
+        pltpu.SemaphoreType.DMA((2,)),
         pltpu.SemaphoreType.DMA(()),
     )
 

time: 380 us -> 372 us (0.979)
  Pallas kernels: 373 us -> 366 us
    pallas_call x1, Pallas kernels: 373 us -> 366 us  [device_step(): pl.pallas_call(functools.partial(layer_kernel, (groups, tokens, dim, hid,...]
where the time goes in v2:
time: 372 us; the launch traced here: 371 us
  Pallas kernels  366 us (98%)
  local copies, waits for them, and re-layouts  4.83 us (1%)
    pallas_call x1, Pallas kernels, device_step(): pl.pallas_call(functools.partial(layer_kernel, (groups, tokens, dim, hid,...  366 us

profile of v2, /device:TPU:81, one launch (start us, length us, event | category | flops | bytes accessed | tf_op | source)
XLA Modules:
  0.0 371.2 jit_solution(17592154822814544477)
XLA Ops:
  0.0 366.4 %layer.1 = (bf16[1024,2304]{1,0:T(8,128)(2,1)}, bf16[8,1024,2304]{2,1,0:T(8,128)(2,1)}, bf16[8,448,2304]{2,1,0:T(8,128)(2,1)}, bf16[8,448,2304]{2,1,0:T(8,128)(2,1)}) custom-call(bf16[1024,2304]{1,0:T(8,128)(2,1)} %x_ref.1, s32[2,1024]{1,0:T(2,128)} %bitcast.6, f32[2,1024]{1,0:T(2,128)} %bitcast.7, bf16[2304,5760]{1,0:T(8,128)(2,1)} %bitcast.4, ...), custom_call_target="tpu_custom_call" | custom-call | flops 190253629440 | bytes 400000000 | tf_op jit(solution)/shard_map/layer/pallas_call | solution.py:416
  366.4 4.8 %copy.7 = bf16[1024,2304]{1,0:T(8,128)(2,1)} copy(bf16[1024,2304]{1,0:T(8,128)(2,1)} %get-tuple-element.6) | data formatting | bytes 9437184

commit v3 on v2

--- a/solution.py
+++ b/solution.py
@@ -12,8 +12,8 @@
 BF16 = jnp.bfloat16
 
 
-def layer_kernel(cfg, x_ref, ids_ref, gates_ref, win_ref, wout_ref, out_ref, ag_ref, obuf_ref, rbuf_ref,
-                 ids_all, slot_tab, comb_tab, ids_send, ids_recv, ag_send, ag_recv, ret_send, ret_recv, barrier_unused=None):
+def layer_kernel(cfg, x_ref, ids_ref, gates_ref, win_ref, wout_ref, acc_ref, tab_ref, rfar_ref, ag_ref, obuf_ref, rbuf_ref,
+                 ids_all, slot_tab, comb_tab, ids_send, ids_recv, ag_send, ag_recv, ret_send, ret_recv):
     groups, tokens, dim, hid, cap, slots = cfg
     half = tokens // 2
     chips = groups // 2
@@ -99,12 +99,20 @@
         d = tile_dev(t, 1)
         return remote(obuf_ref.at[d], rbuf_ref.at[me], ret_send.at[t], ret_recv.at[me], d)
 
+    def ret_far(p):
+        d = dev(2, core * (1 - p) + other * p)
+        return remote(obuf_ref.at[d], rfar_ref.at[core], ret_send.at[groups - 2 + p], ret_recv.at[me], d)
+
     for k in range(1, groups):
         ids_copy(k).start()
     for c in send_sib + send_a:
         c.start()
 
-    def compute(xsrc, xg, hbuf, pact, wbuf, wout, ostage, pbuf, xsem, wsem, osem, stsem, isem):
+    def compute(xsrc, xg, hbuf, pact, wbuf, wout, pbuf, xsem, wsem, osem, stsem, isem):
+        passes = groups // 2
+        ochunk = 512
+        ofull = dim // ochunk
+        otail = dim - ofull * ochunk
         own_ids = pltpu.make_async_copy(ids_ref, ids_all.at[me], isem)
         own_ids.start()
 
@@ -113,12 +121,14 @@
 
         win_tail = pltpu.make_async_copy(win_ref.at[:, pl.ds(nfull * wchunk, tail)], wbuf.at[nfull % 2, :, pl.ds(0, tail)], wsem.at[nfull % 2])
 
-        def wout_part(n):
-            return pltpu.make_async_copy(wout_ref.at[:, pl.ds(pl.multiple_of(n * wchunk, 128), wchunk)], wout.at[:, pl.ds(pl.multiple_of(n * wchunk, 128), wchunk)], osem.at[n])
+        def wout_part(n, g):
+            return pltpu.make_async_copy(wout_ref.at[:, pl.ds(pl.multiple_of(n * ochunk, 128), ochunk)], wout.at[g % 2], osem.at[g % 2])
+
+        def wout_tail(g):
+            return pltpu.make_async_copy(wout_ref.at[:, pl.ds(ofull * ochunk, otail)], wout.at[g % 2, :, pl.ds(0, otail)], osem.at[g % 2])
 
         win_full(0).start()
-        for n in range(ochunks):
-            wout_part(n).start()
+        wout_part(0, 0).start()
 
         own_ids.wait()
         for k in range(1, groups):
@@ -140,8 +150,12 @@
         n0 = ind(o0 == eidx)
         n1 = ind(o1 == eidx)
         stack = jnp.concatenate([m0, m1, n0, n1], axis=0).astype(BF16)
-        tri = ind(lax.broadcasted_iota(jnp.int32, (tokens, tokens), 0) < lax.broadcasted_iota(jnp.int32, (tokens, tokens), 1)).astype(BF16)
-        pre = jnp.dot(stack, tri, preferred_element_type=F32)
+        parts = []
+        for h in range(2):
+            earlier = lax.broadcasted_iota(jnp.int32, (tokens, half), 0) < lax.broadcasted_iota(jnp.int32, (tokens, half), 1) + h * half
+            xsrc[h, :, 0:half] = ind(earlier).astype(BF16)
+            parts.append(jnp.dot(stack, xsrc[h, :, 0:half], preferred_element_type=F32))
+        pre = jnp.concatenate(parts, axis=1)
         s0, s1, r0, r1 = [pre[k * groups:(k + 1) * groups] for k in range(4)]
         c0 = jnp.sum(m0, axis=1, keepdims=True)
         c1 = jnp.sum(m1, axis=1, keepdims=True)
@@ -173,144 +187,187 @@
         own1 = jnp.logical_and(n1 > 0, jnp.concatenate(g1, axis=0) + r1 < cap)
         slot_own = jnp.where(own0, r0, jnp.where(own1, k0 + r1, -1.0))
         gate_own = n0 * gates_ref[0:1, :] + n1 * gates_ref[1:2, :]
-        both = jnp.concatenate([slot_own, gate_own, jnp.zeros((128 - 2 * groups, tokens), F32)], axis=0)
+        far_rows = []
+        for v in (slot_own, gate_own):
+            for b in range(2):
+                far_rows.append(jnp.sum(jnp.where(eidx == dev(2, b), v, 0.0), axis=0, keepdims=True))
+        both = jnp.concatenate([slot_own, gate_own] + far_rows + [jnp.zeros((124 - 2 * groups, tokens), F32)], axis=0)
         comb_tab[...] = jnp.transpose(both)
 
-        def stage_copy_own():
-            return pltpu.make_async_copy(ostage, rbuf_ref.at[me], stsem)
-
-        def stage_copy(t):
-            return pltpu.make_async_copy(ostage, obuf_ref.at[tile_dev(t, 1)], stsem)
-
-        def tile(t, carry):
-            d = tile_dev(t, 1)
-
-            @pl.when(t % 2 == 1)
-            def _():
-                wait_half(d, 0)
-                wait_half(d, 1)
-
-            def xcols(n):
-                return pl.ds(pl.multiple_of(n * wchunk, 128), wchunk)
-
-            def x_start(n):
-                @pl.when(t == 0)
-                def _():
-                    pltpu.make_async_copy(x_ref.at[:, xcols(n)], xsrc.at[n % 2], xsem.at[n % 2]).start()
-
-                @pl.when(t > 0)
-                def _():
-                    pltpu.make_async_copy(ag_ref.at[d, :, xcols(n)], xsrc.at[n % 2], xsem.at[n % 2]).start()
+        def stage_rows(p):
+            return xg.at[pl.ds(p * slots, slots)]
+
+        def stage_own():
+            return pltpu.make_async_copy(stage_rows(0), rbuf_ref.at[me], stsem.at[0])
+
+        def stage_copy(q, p):
+            return pltpu.make_async_copy(stage_rows(p), obuf_ref.at[tile_dev(2 * q + p, 1)], stsem.at[p])
+
+        def xcols(n):
+            return pl.ds(pl.multiple_of(n * wchunk, 128), wchunk)
+
+        def one_pass(q, carry):
+            wait_half(tile_dev(2 * q + 1, 1), 0)
+            wait_half(tile_dev(2 * q + 1, 1), 1)
+
+            def x_start(m):
+                p = m // ochunks
+                n = m % ochunks
+                own = jnp.logical_and(q == 0, p == 0)
+
+                @pl.when(own)
+                def _():
+                    pltpu.make_async_copy(x_ref.at[:, xcols(n)], xsrc.at[m % 2], xsem.at[m % 2]).start()
+
+                @pl.when(jnp.logical_not(own))
+                def _():
+                    pltpu.make_async_copy(ag_ref.at[tile_dev(2 * q + p, 1), :, xcols(n)], xsrc.at[m % 2], xsem.at[m % 2]).start()
 
             x_start(0)
-            row = slot_tab[pl.ds(d, 1), :]
-            pbuf[...] = jnp.where(lax.broadcasted_iota(jnp.int32, (slots, tokens), 0).astype(F32) == row, 1.0, 0.0).astype(BF16)
-
-            def gather(n, cc):
-                @pl.when(n + 1 < ochunks)
-                def _():
-                    x_start(n + 1)
-                pltpu.make_async_copy(x_ref.at[:, xcols(n)], xsrc.at[n % 2], xsem.at[n % 2]).wait()
-                xg[:, xcols(n)] = jnp.dot(pbuf[...], xsrc[n % 2], preferred_element_type=F32).astype(BF16)
+
+            @pl.when(q == 1)
+            def _():
+                stage_own().wait()
+
+            @pl.when(q > 1)
+            def _():
+                stage_copy(q - 1, 0).wait()
+                ret_copy(2 * q - 2).start()
+
+            @pl.when(q > 0)
+            def _():
+                stage_copy(q - 1, 1).wait()
+                ret_copy(2 * q - 1).start()
+
+            def gather_block(p, c1):
+                row = slot_tab[pl.ds(tile_dev(2 * q + p, 1), 1), :]
+                pbuf[...] = jnp.where(lax.broadcasted_iota(jnp.int32, (slots, tokens), 0).astype(F32) == row, 1.0, 0.0).astype(BF16)
+                rows = pl.ds(pl.multiple_of(p * slots, slots), slots)
+
+                def gather(n, c2):
+                    m = p * ochunks + n
+
+                    @pl.when(m + 1 < 2 * ochunks)
+                    def _():
+                        x_start(m + 1)
+                    pltpu.make_async_copy(x_ref.at[:, xcols(n)], xsrc.at[m % 2], xsem.at[m % 2]).wait()
+                    xg[rows, xcols(n)] = jnp.dot(pbuf[...], xsrc[m % 2], preferred_element_type=F32).astype(BF16)
+                    return c2
+
+                return lax.fori_loop(0, ochunks, gather, c1)
+
+            lax.fori_loop(0, 2, gather_block, 0)
+
+            def up(i, cc):
+                @pl.when(i + 1 < nfull)
+                def _():
+                    win_full(i + 1).start()
+
+                @pl.when(i + 1 == nfull)
+                def _():
+                    win_tail.start()
+
+                win_full(i).wait()
+                hbuf[:, xcols(i - 1)] = jax.nn.gelu(pact[...]).astype(BF16)
+                pact[...] = jnp.dot(xg[...], wbuf[i % 2], preferred_element_type=F32)
                 return cc
 
-            lax.fori_loop(0, ochunks, gather, 0)
-
-            def up(i, cc):
-                @pl.when(jnp.logical_and(t == 1, i == 2))
-                def _():
-                    stage_copy_own().wait()
+            win_full(1).start()
+            win_full(0).wait()
+            pact[...] = jnp.dot(xg[...], wbuf[0], preferred_element_type=F32)
+            lax.fori_loop(1, nfull, up, 0)
+            win_tail.wait()
+
+            @pl.when(q + 1 < passes)
+            def _():
+                win_full(0).start()
+            hbuf[:, (nfull - 1) * wchunk:nfull * wchunk] = jax.nn.gelu(pact[...]).astype(BF16)
+            pre_act = jnp.dot(xg[...], wbuf[nfull % 2, :, 0:tail], preferred_element_type=F32)
+            hbuf[:, nfull * wchunk:hid] = jax.nn.gelu(pre_act).astype(BF16)
+
+            def down(n, cc):
+                g = q * (ofull + 1) + n
+
+                @pl.when(n + 1 < ofull)
+                def _():
+                    wout_part(n + 1, g + 1).start()
+
+                @pl.when(n + 1 == ofull)
+                def _():
+                    wout_tail(g + 1).start()
+
+                @pl.when(jnp.logical_and(q == 0, n == 0))
+                def _():
                     wait_half(src_a, 0)
                     pass_a[0].start()
 
-                @pl.when(jnp.logical_and(t == 3, i == 3))
-                def _():
-                    wait_half(src_b, half_b)
-                    fwd_b.start()
-                    pass_b1.start()
-
-                @pl.when(jnp.logical_and(t == 4, i == 3))
-                def _():
-                    wait_half(far, half_a)
-                    pass_f1.start()
-
-                @pl.when(jnp.logical_and(t > 1, i == 1))
-                def _():
-                    stage_copy(t - 1).wait()
-
-                    @pl.when(t != 3)
-                    def _():
-                        ret_copy(t - 1).start()
-
-                @pl.when(i + 1 < nfull)
-                def _():
-                    win_full(i + 1).start()
-
-                @pl.when(i + 1 == nfull)
-                def _():
-                    win_tail.start()
-
-                win_full(i).wait()
-                prev = pl.ds(pl.multiple_of((i - 1) * wchunk, 128), wchunk)
-                hbuf[:, prev] = jax.nn.gelu(pact[(i - 1) % 2]).astype(BF16)
-                pact[i % 2] = jnp.dot(xg[...], wbuf[i % 2], preferred_element_type=F32)
-                return cc
-
-            win_full(1).start()
-            win_full(0).wait()
-            pact[0] = jnp.dot(xg[...], wbuf[0], preferred_element_type=F32)
-            lax.fori_loop(1, nfull, up, 0)
-            win_tail.wait()
-
-            @pl.when(t + 1 < groups)
-            def _():
-                win_full(0).start()
-            hbuf[:, (nfull - 1) * wchunk:nfull * wchunk] = jax.nn.gelu(pact[(nfull - 1) % 2]).astype(BF16)
-            pre_act = jnp.dot(xg[...], wbuf[nfull % 2, :, 0:tail], preferred_element_type=F32)
-            hbuf[:, nfull * wchunk:hid] = jax.nn.gelu(pre_act).astype(BF16)
-
-            def down(n, cc):
-                @pl.when(t == 0)
-                def _():
-                    wout_part(n).wait()
-
-                @pl.when(jnp.logical_and(t == 1, n == 0))
+                @pl.when(jnp.logical_and(q == 0, n == 3))
                 def _():
                     send_b1.start()
                     send_b2.start()
                     wait_half(src_a, 1)
+                    pass_a[1].start()
+
+                @pl.when(jnp.logical_and(q == 1, n == 0))
+                def _():
+                    wait_half(src_b, half_b)
+                    pass_b1.start()
+
+                @pl.when(jnp.logical_and(q == 1, n == 2))
+                def _():
                     fwd_a.start()
-                    pass_a[1].start()
-
-                @pl.when(jnp.logical_and(t == 3, n == 2))
+                    fwd_b.start()
+
+                @pl.when(jnp.logical_and(q == 1, n == 3))
                 def _():
                     wait_half(src_b, half_a)
                     pass_b2.start()
-                    ret_copy(2).start()
-
-                @pl.when(jnp.logical_and(t == 5, n == 0))
-                def _():
+
+                @pl.when(jnp.logical_and(q == 2, n == 3))
+                def _():
+                    wait_half(far, half_a)
+                    pass_f1.start()
                     wait_half(far, half_b)
                     pass_f2.start()
 
-                cols = pl.ds(pl.multiple_of(n * wchunk, 128), wchunk)
-                ostage[:, cols] = jnp.dot(hbuf[...], wout[:, cols], preferred_element_type=F32).astype(BF16)
-                return cc
-
-            lax.fori_loop(0, ochunks, down, 0)
-
-            @pl.when(t == 0)
-            def _():
-                stage_copy_own().start()
-
-            @pl.when(t > 0)
-            def _():
-                stage_copy(t).start()
+                wout_part(n, g).wait()
+
+                def block(p, c2):
+                    rows = pl.ds(pl.multiple_of(p * slots, slots), slots)
+                    xg[rows, pl.ds(pl.multiple_of(n * ochunk, 128), ochunk)] = jnp.dot(hbuf[rows, :], wout[g % 2], preferred_element_type=F32).astype(BF16)
+                    return c2
+
+                return lax.fori_loop(0, 2, block, cc)
+
+            lax.fori_loop(0, ofull, down, 0)
+            last = q * (ofull + 1) + ofull
+
+            @pl.when(q + 1 < passes)
+            def _():
+                wout_part(0, last + 1).start()
+            wout_tail(last).wait()
+
+            def block_tail(p, c2):
+                rows = pl.ds(pl.multiple_of(p * slots, slots), slots)
+                xg[rows, ofull * ochunk:dim] = jnp.dot(hbuf[rows, :], wout[last % 2, :, 0:otail], preferred_element_type=F32).astype(BF16)
+                return c2
+
+            lax.fori_loop(0, 2, block_tail, 0)
+
+            @pl.when(q == 0)
+            def _():
+                stage_own().start()
+
+            @pl.when(q > 0)
+            def _():
+                stage_copy(q, 0).start()
+            stage_copy(q, 1).start()
             return carry
 
-        lax.fori_loop(0, groups, tile, 0)
-        stage_copy(groups - 1).wait()
-        ret_copy(groups - 1).start()
+        lax.fori_loop(0, passes, one_pass, 0)
+        for p in range(2):
+            stage_copy(passes - 1, p).wait()
+            ret_far(p).start()
 
     def ids_ref_v(ref, d, j):
         return ref[pl.ds(d, 1), j, :]
@@ -318,21 +375,23 @@
     pl.run_scoped(
         compute,
         pltpu.VMEM((2, tokens, wchunk), BF16),
-        pltpu.VMEM((slots, dim), BF16),
-        pltpu.VMEM((slots, hid), BF16),
-        pltpu.VMEM((2, slots, wchunk), F32),
+        pltpu.VMEM((2 * slots, dim), BF16),
+        pltpu.VMEM((2 * slots, hid), BF16),
+        pltpu.VMEM((2 * slots, wchunk), F32),
         pltpu.VMEM((2, dim, wchunk), BF16),
-        pltpu.VMEM((hid, dim), BF16),
-        pltpu.VMEM((slots, dim), BF16),
+        pltpu.VMEM((2, hid, 512), BF16),
         pltpu.VMEM((slots, tokens), BF16),
         pltpu.SemaphoreType.DMA((2,)),
         pltpu.SemaphoreType.DMA((2,)),
-        pltpu.SemaphoreType.DMA((ochunks,)),
-        pltpu.SemaphoreType.DMA(()),
+        pltpu.SemaphoreType.DMA((2,)),
+        pltpu.SemaphoreType.DMA((2,)),
         pltpu.SemaphoreType.DMA(()),
     )
 
     def combine(acc, xb, rb, qbuf, xsem, rsem, osem):
+        near = groups - 2
+        tab_out = pltpu.make_async_copy(comb_tab, tab_ref, osem.at[1])
+        tab_out.start()
         x_in = pltpu.make_async_copy(x_ref, xb, xsem)
         x_in.start()
         x_in.wait()
@@ -353,7 +412,7 @@
         def add_block(k, cc):
             e = comb_dev(k)
 
-            @pl.when(k < groups - 2)
+            @pl.when(k + 1 < near)
             def _():
                 block_ready(k + 1)
             lane = lax.broadcasted_iota(jnp.int32, (tokens, 128), 1)
@@ -369,18 +428,13 @@
                 acc[:, cols] = acc[:, cols] + gate_col * pick
                 return c2
 
-            lax.fori_loop(0, ochunks, part, 0)
-
-            @pl.when(k == groups - 2)
-            def _():
-                block_ready(k + 1)
-            return cc
-
-        lax.fori_loop(0, groups, add_block, 0)
-        xb[...] = acc[...].astype(BF16)
-        fin = pltpu.make_async_copy(xb, out_ref, osem)
+            return lax.fori_loop(0, ochunks, part, cc)
+
+        lax.fori_loop(0, near, add_block, 0)
+        fin = pltpu.make_async_copy(acc, acc_ref, osem.at[0])
         fin.start()
         fin.wait()
+        tab_out.wait()
 
     pl.run_scoped(
         combine,
@@ -390,13 +444,27 @@
         pltpu.VMEM((tokens, slots), BF16),
         pltpu.SemaphoreType.DMA(()),
         pltpu.SemaphoreType.DMA((2,)),
-        pltpu.SemaphoreType.DMA(()),
+        pltpu.SemaphoreType.DMA((2,)),
     )
 
     for c in all_sends:
         c.wait_send()
-    for t in range(1, groups):
+    for t in range(1, groups - 2):
         ret_copy(t).wait_send()
+    for p in range(2):
+        ret_far(p).wait_send()
+        remote(obuf_ref.at[me], rfar_ref.at[p], ret_send.at[0], ret_recv.at[dev(2, p)], sib).wait_recv()
+
+
+def finish_kernel(base, acc_ref, tab_ref, rfar_ref, out_ref):
+    rows, dim = out_ref.shape
+    slots = rfar_ref.shape[1]
+    total = acc_ref[...]
+    col = lax.broadcasted_iota(jnp.int32, (rows, slots), 1).astype(F32)
+    for b in range(2):
+        pick = jnp.where(col == tab_ref[:, base + b:base + b + 1], 1.0, 0.0).astype(BF16)
+        total = total + tab_ref[:, base + 2 + b:base + 3 + b] * jnp.dot(pick, rfar_ref[b], preferred_element_type=F32)
+    out_ref[...] = total.astype(BF16)
 
 
 def solution(mesh):
@@ -413,16 +481,18 @@
         any_spec = pl.BlockSpec(memory_space=pl.ANY)
         vmem_spec = pl.BlockSpec(memory_space=pltpu.VMEM)
         flops = 4 * groups * slots * dim * hid
-        out = pl.pallas_call(
+        acc, tab, rfar = pl.pallas_call(
             functools.partial(layer_kernel, (groups, tokens, dim, hid, cap, slots)),
             out_shape=(
-                jax.ShapeDtypeStruct((tokens, dim), BF16),
+                jax.ShapeDtypeStruct((tokens, dim), F32),
+                jax.ShapeDtypeStruct((tokens, 128), F32),
+                jax.ShapeDtypeStruct((2, slots, dim), BF16),
                 jax.ShapeDtypeStruct((groups, tokens, dim), BF16),
                 jax.ShapeDtypeStruct((groups, slots, dim), BF16),
                 jax.ShapeDtypeStruct((groups, slots, dim), BF16),
             ),
             in_specs=[any_spec, any_spec, vmem_spec, any_spec, any_spec],
-            out_specs=(any_spec, any_spec, any_spec, any_spec),
+            out_specs=(any_spec,) * 6,
             scratch_shapes=[
                 pltpu.VMEM((groups, top_k, tokens), jnp.int32),
                 pltpu.VMEM((groups, tokens), F32),
@@ -437,7 +507,20 @@
             compiler_params=pltpu.CompilerParams(collective_id=0, has_side_effects=True, vmem_limit_bytes=67043328),
             cost_estimate=pl.CostEstimate(flops=flops, bytes_accessed=400000000, transcendentals=0),
             name="layer",
-        )(token_rows, expert_ids.T, gate_weights.T, w_in.reshape(dim, hid), w_out.reshape(hid, dim))
-        return out[0]
+        )(token_rows, expert_ids.T, gate_weights.T, w_in.reshape(dim, hid), w_out.reshape(hid, dim))[:3]
+        rows = tokens // 4
+        return pl.pallas_call(
+            functools.partial(finish_kernel, 2 * groups),
+            grid=(tokens // rows,),
+            in_specs=[
+                pl.BlockSpec((rows, dim), lambda i: (i, 0)),
+                pl.BlockSpec((rows, 128), lambda i: (i, 0)),
+                pl.BlockSpec((2, slots, dim), lambda i: (0, 0, 0)),
+            ],
+            out_specs=pl.BlockSpec((rows, dim), lambda i: (i, 0)),
+            out_shape=jax.ShapeDtypeStruct((tokens, dim), BF16),
+            cost_estimate=pl.CostEstimate(flops=4 * tokens * slots * dim, bytes_accessed=20000000, transcendentals=0),
+            name="finish",
+        )(acc, tab, rfar)
 
     return jax.shard_map(device_step, mesh=mesh, in_specs=(row_spec, row_spec, row_spec, weight_spec, weight_spec), out_specs=row_spec, check_vma=False)

time: 372 us -> 377 us (1.013)
  Pallas kernels: 366 us -> 376 us
  local copies, waits for them, and re-layouts: 4.83 us -> 0 us
    pallas_call x0 -> x1, Pallas kernels: none -> 11.4 us  [device_step(): pl.pallas_call(functools.partial(finish_kernel, 2 * groups), grid=(tokens...]
    unnamed x1 -> x0, local copies, waits for them, and re-layouts: 4.83 us -> none
where the time goes in v3:
time: 377 us; the launch traced here: 376 us
  Pallas kernels  376 us (100%)
    pallas_call x1, Pallas kernels, device_step(): pl.pallas_call(functools.partial(layer_kernel, (groups, tokens, dim, hid,...  365 us
    pallas_call x1, Pallas kernels, device_step(): pl.pallas_call(functools.partial(finish_kernel, 2 * groups), grid=(tokens...  11.4 us

profile of v3, /device:TPU:81, one launch (start us, length us, event | category | flops | bytes accessed | tf_op | source)
XLA Modules:
  0.0 376.3 jit_solution(3906861661207609433)
XLA Ops:
  0.0 365.0 %layer.1 = (f32[1024,2304]{1,0:T(8,128)}, f32[1024,128]{1,0:T(8,128)}, bf16[2,448,2304]{2,1,0:T(8,128)(2,1)}, bf16[8,1024,2304]{2,1,0:T(8,128)(2,1)}, bf16[8,448...) custom-call(bf16[1024,2304]{1,0:T(8,128)(2,1)} %x_ref.1, s32[2,1024]{1,0:T(2,128)} %bitcast.6, f32[2,1024]{1,0:T(2,128)} %bitcast.7, ...), custom_call_target="tpu_custom_call" | custom-call | flops 190253629440 | bytes 400000000 | tf_op jit(solution)/shard_map/layer/pallas_call | solution.py:484
  365.0 11.4 %finish.1 = bf16[1024,2304]{1,0:T(8,128)(2,1)} custom-call(f32[1024,2304]{1,0:T(8,128)} %get-tuple-element.8.acc_ref, f32[1024,128]{1,0:T(8,128)} %get-tuple-element.9.tab_ref, bf16[2,448,2304]{2,1,0:T(8,128)(2,1)} %get-tuple-element.10.rfar_ref), custom_call_target="tpu_custom_call" | custom-call | flops 4227858432 | bytes 20000000 | tf_op jit(solution)/shard_map/finish/pallas_call | solution.py:512

commit v4 on v2

--- a/solution.py
+++ b/solution.py
@@ -55,6 +55,10 @@
         off = (f1 - f2) * sgn + 2 * f3
         c = core * (1 - p) + other * p
         return dev(off, c)
+
+    def order(s):
+        late = s // 5
+        return s * (1 - late) + late * (5 + (s + 2) % 3)
 
     def remote(src, dst, ssem, rsem, target):
         return pltpu.make_async_remote_copy(src_ref=src, dst_ref=dst, send_sem=ssem, recv_sem=rsem,
@@ -182,7 +186,8 @@
         def stage_copy(t):
             return pltpu.make_async_copy(ostage, obuf_ref.at[tile_dev(t, 1)], stsem)
 
-        def tile(t, carry):
+        def tile(s, carry):
+            t = order(s)
             d = tile_dev(t, 1)
 
             @pl.when(t % 2 == 1)
@@ -194,11 +199,11 @@
                 return pl.ds(pl.multiple_of(n * wchunk, 128), wchunk)
 
             def x_start(n):
-                @pl.when(t == 0)
+                @pl.when(s == 0)
                 def _():
                     pltpu.make_async_copy(x_ref.at[:, xcols(n)], xsrc.at[n % 2], xsem.at[n % 2]).start()
 
-                @pl.when(t > 0)
+                @pl.when(s > 0)
                 def _():
                     pltpu.make_async_copy(ag_ref.at[d, :, xcols(n)], xsrc.at[n % 2], xsem.at[n % 2]).start()
 
@@ -217,30 +222,30 @@
             lax.fori_loop(0, ochunks, gather, 0)
 
             def up(i, cc):
-                @pl.when(jnp.logical_and(t == 1, i == 2))
+                @pl.when(jnp.logical_and(s == 1, i == 2))
                 def _():
                     stage_copy_own().wait()
                     wait_half(src_a, 0)
                     pass_a[0].start()
 
-                @pl.when(jnp.logical_and(t == 3, i == 3))
+                @pl.when(jnp.logical_and(s == 3, i == 3))
                 def _():
                     wait_half(src_b, half_b)
                     fwd_b.start()
                     pass_b1.start()
 
-                @pl.when(jnp.logical_and(t == 4, i == 3))
+                @pl.when(jnp.logical_and(s == 4, i == 3))
                 def _():
                     wait_half(far, half_a)
                     pass_f1.start()
 
-                @pl.when(jnp.logical_and(t > 1, i == 1))
-                def _():
-                    stage_copy(t - 1).wait()
-
-                    @pl.when(t != 3)
+                @pl.when(jnp.logical_and(s > 1, i == 1))
+                def _():
+                    stage_copy(order(s - 1)).wait()
+
+                    @pl.when(s != 3)
                     def _():
-                        ret_copy(t - 1).start()
+                        ret_copy(order(s - 1)).start()
 
                 @pl.when(i + 1 < nfull)
                 def _():
@@ -262,7 +267,7 @@
             lax.fori_loop(1, nfull, up, 0)
             win_tail.wait()
 
-            @pl.when(t + 1 < groups)
+            @pl.when(s + 1 < groups)
             def _():
                 win_full(0).start()
             hbuf[:, (nfull - 1) * wchunk:nfull * wchunk] = jax.nn.gelu(pact[(nfull - 1) % 2]).astype(BF16)
@@ -270,11 +275,11 @@
             hbuf[:, nfull * wchunk:hid] = jax.nn.gelu(pre_act).astype(BF16)
 
             def down(n, cc):
-                @pl.when(t == 0)
+                @pl.when(s == 0)
                 def _():
                     wout_part(n).wait()
 
-                @pl.when(jnp.logical_and(t == 1, n == 0))
+                @pl.when(jnp.logical_and(s == 1, n == 0))
                 def _():
                     send_b1.start()
                     send_b2.start()
@@ -282,13 +287,13 @@
                     fwd_a.start()
                     pass_a[1].start()
 
-                @pl.when(jnp.logical_and(t == 3, n == 2))
+                @pl.when(jnp.logical_and(s == 3, n == 2))
                 def _():
                     wait_half(src_b, half_a)
                     pass_b2.start()
                     ret_copy(2).start()
 
-                @pl.when(jnp.logical_and(t == 5, n == 0))
+                @pl.when(jnp.logical_and(s == 4, n == 0))
                 def _():
                     wait_half(far, half_b)
                     pass_f2.start()
@@ -299,18 +304,18 @@
 
             lax.fori_loop(0, ochunks, down, 0)
 
-            @pl.when(t == 0)
+            @pl.when(s == 0)
             def _():
                 stage_copy_own().start()
 
-            @pl.when(t > 0)
+            @pl.when(s > 0)
             def _():
                 stage_copy(t).start()
             return carry
 
         lax.fori_loop(0, groups, tile, 0)
-        stage_copy(groups - 1).wait()
-        ret_copy(groups - 1).start()
+        stage_copy(order(groups - 1)).wait()
+        ret_copy(order(groups - 1)).start()
 
     def ids_ref_v(ref, d, j):
         return ref[pl.ds(d, 1), j, :]
@@ -341,17 +346,17 @@
             acc[:, cols] = xb[:, cols].astype(F32)
 
         def block_copy(k):
-            return pltpu.make_async_copy(rbuf_ref.at[comb_dev(k)], rb.at[k % 2], rsem.at[k % 2])
+            return pltpu.make_async_copy(rbuf_ref.at[comb_dev(order(k))], rb.at[k % 2], rsem.at[k % 2])
 
         def block_ready(k):
-            e = comb_dev(k)
+            e = comb_dev(order(k))
             remote(obuf_ref.at[e], rbuf_ref.at[e], ret_send.at[0], ret_recv.at[e], sib).wait_recv()
             block_copy(k).start()
 
         block_copy(0).start()
 
         def add_block(k, cc):
-            e = comb_dev(k)
+            e = comb_dev(order(k))
 
             @pl.when(k < groups - 2)
             def _():

time: 372 us -> 366 us (0.984)
  Pallas kernels: 366 us -> 360 us
    pallas_call x1, Pallas kernels: 366 us -> 360 us  [device_step(): pl.pallas_call(functools.partial(layer_kernel, (groups, tokens, dim, hid,...]
where the time goes in v4:
time: 366 us; the launch traced here: 365 us
  Pallas kernels  360 us (98%)
  local copies, waits for them, and re-layouts  4.83 us (1%)
    pallas_call x1, Pallas kernels, device_step(): pl.pallas_call(functools.partial(layer_kernel, (groups, tokens, dim, hid,...  360 us

profile of v4, /device:TPU:81, one launch (start us, length us, event | category | flops | bytes accessed | tf_op | source)
XLA Modules:
  0.0 364.8 jit_solution(4065997218568669546)
XLA Ops:
  0.0 360.0 %layer.1 = (bf16[1024,2304]{1,0:T(8,128)(2,1)}, bf16[8,1024,2304]{2,1,0:T(8,128)(2,1)}, bf16[8,448,2304]{2,1,0:T(8,128)(2,1)}, bf16[8,448,2304]{2,1,0:T(8,128)(2,1)}) custom-call(bf16[1024,2304]{1,0:T(8,128)(2,1)} %x_ref.1, s32[2,1024]{1,0:T(2,128)} %bitcast.6, f32[2,1024]{1,0:T(2,128)} %bitcast.7, bf16[2304,5760]{1,0:T(8,128)(2,1)} %bitcast.4, ...), custom_call_target="tpu_custom_call" | custom-call | flops 190253629440 | bytes 400000000 | tf_op jit(solution)/shard_map/layer/pallas_call | solution.py:421
  360.0 4.8 %copy.7 = bf16[1024,2304]{1,0:T(8,128)(2,1)} copy(bf16[1024,2304]{1,0:T(8,128)(2,1)} %get-tuple-element.6) | data formatting | bytes 9437184
